TPU v7x, 32 devices: a whole 2x2x4 slice. The times are simulated.
32 devices in a mesh: grp: 8 (over y, x, core), mem: 4 (over z).
Axes of the slice: x: 2, y: 2, z: 4, core: 2. Of those that a mesh axis runs over, the one named last changes fastest.
Arguments:
- inverse: bfloat16 [64, 2048, 2048], P(('grp', 'mem')), may hold values from -0.125 to 0.125
- sources: bfloat16 [64, 2048, 256], P(('grp', 'mem')), may hold values from -6 to 6
- slot_blocks: int32 [32, 20], P(('grp', 'mem')), may hold values from -1 to 31, as said below
Outputs:
- controls: float32 [32, 20, 32768], P(('grp', 'mem'))
- states: bfloat16 [64, 2048, 256], P(('grp', 'mem'))
Inputs may be any that keep to these rules, and one draw needn't show every extreme that they name: `slot_blocks`: slots pair up: slot s of a device and the slot named its partner are both empty or both filled. Toward each neighbouring cluster a device fills its first slots, from 1 to 6 of them; toward each other device of its cluster its first 1 to 2 slots; toward itself none. 6 and 2 are reached in every draw. Several slots may name one position.
All inputs are finite; a program needn't handle non-finite values.
Results may differ from a plain program's by a relative error of at most 0.004.
Values may be sent and summed in bfloat16 or wider, within the bound.
A program may use at most 128 MiB of HBM per device.

v0:
```python
import functools

import jax
import jax.numpy as jnp
from jax import lax
from jax.experimental import pallas as pl
from jax.experimental.pallas import tpu as pltpu
from jax.sharding import PartitionSpec as P

BLOCK = 128
CAP = 6
CAPM = 2
PENALTY = 0.5
F32 = jnp.float32
BF16 = jnp.bfloat16
MESH = pl.DeviceIdType.MESH


def kernel(
    sizes, table, inv_hbm, src_hbm, ctl_ref, out_ref,
    a, kmat, src, s0, v, vt, vm, g, h, d, mom, recv, red1, red2,
    load_sem, src_sem, send_sem, recv_sem, r1s, r1r, r2s, r2r,
):
    groups, members, tiles, near, slots = sizes
    width = s0.shape[2]
    nblocks, per = a.shape[:2]
    order = per * BLOCK
    live_slots = slots - CAPM
    rows = live_slots * BLOCK
    gi = lax.axis_index("grp")
    mi = lax.axis_index("mem")

    step_blocks = nblocks // tiles
    in_frac = per // step_blocks

    src_copy = pltpu.make_async_copy(src_hbm, src, src_sem)
    src_copy.start()

    def load(i, carry):
        f, r = lax.div(i, in_frac), lax.rem(i, in_frac)
        for j in range(per):
            pltpu.make_async_copy(
                inv_hbm.at[f, pl.ds(r * step_blocks, step_blocks), :, pl.ds(j * BLOCK, BLOCK)],
                a.at[pl.ds(i * step_blocks, step_blocks), j],
                load_sem.at[i],
            ).start()
        return carry

    lax.fori_loop(0, tiles, load, 0)

    barrier = pltpu.get_barrier_semaphore()
    for k in range(1, groups):
        pl.semaphore_signal(barrier, inc=1, device_id={"grp": lax.rem(gi + k, groups)}, device_id_type=MESH)
    for k in range(1, members):
        pl.semaphore_signal(barrier, inc=1, device_id={"mem": lax.rem(mi + k, members)}, device_id_type=MESH)

    def full_slot(c):
        j = (c - 2 * near) // CAPM
        k = (c - 2 * near) % CAPM
        return 2 * near + lax.rem(mi + 1 + j, members) * CAPM + k

    names = []
    for c in range(live_slots):
        names.append(table[c] if c < 2 * near else table[full_slot(c)])
    place = [jnp.maximum(t, 0) for t in names]
    frac = [lax.div(t, per) for t in place]
    column = [t - f * per for t, f in zip(place, frac)]
    alive = [(t >= 0).astype(F32) for t in names]

    def exchange(e):
        copies = []
        plan = [
            (0, near, near, {"grp": lax.rem(gi + 1, groups)}),
            (near, 0, near, {"grp": lax.rem(gi + groups - 1, groups)}),
        ]
        for j in range(members - 1):
            plan.append((
                2 * near + j * CAPM,
                2 * near + (members - 2 - j) * CAPM,
                CAPM,
                {"mem": lax.rem(mi + 1 + j, members)},
            ))
        for i, (at, to, count, device) in enumerate(plan):
            copies.append(pltpu.make_async_remote_copy(
                src_ref=mom.at[e, pl.ds(at, count)],
                dst_ref=recv.at[e, pl.ds(to, count)],
                send_sem=send_sem.at[e, i],
                recv_sem=recv_sem.at[e, i],
                device_id=device,
                device_id_type=MESH,
            ))
        return copies, [(to, count) for _, to, count, _ in plan]

    def take(moves, one, carry):
        copies, landed = moves
        for i in (*range(2, members + 1), 0, 1):
            copies[i].wait()
            carry = lax.fori_loop(landed[i][0], landed[i][0] + landed[i][1], one, carry)
        return carry

    src_copy.wait()

    def first(i, carry):
        whole = a.at[pl.ds(i * step_blocks, step_blocks)]
        pltpu.make_async_copy(whole, whole, load_sem.at[i]).wait()
        f = lax.div(i, in_frac)
        lhs = jnp.concatenate(
            [
                a[pl.ds(i * step_blocks, step_blocks), j].reshape(step_blocks * BLOCK, BLOCK)
                for j in range(per)
            ],
            axis=1,
        )
        prod = jnp.dot(lhs, src[f].reshape(order, width), preferred_element_type=F32)
        s0[pl.ds(i * step_blocks, step_blocks)] = prod.reshape(step_blocks, BLOCK, width)
        return carry

    lax.fori_loop(0, tiles, first, 0)

    for c in range(live_slots):
        x = s0[place[c]]
        mom[0, c] = (x * alive[c]).astype(BF16)
    pl.semaphore_wait(barrier, groups - 1 + members - 1)
    moves = exchange(0)
    for copy in (*moves[0][2:], *moves[0][:2]):
        copy.start()

    for r in range(live_slots):
        for c in range(live_slots):
            weight = (frac[r] == frac[c]).astype(F32) * alive[r] * alive[c]
            kmat[pl.ds(r * BLOCK, BLOCK), pl.ds(c * BLOCK, BLOCK)] = a[place[r], column[c]] * jnp.full(
                (BLOCK, BLOCK), weight, F32
            ).astype(BF16)

    def fold(x):
        return jnp.sum(x.reshape(BLOCK // 8, 8, width), axis=0)

    zero = jnp.zeros((8, width), F32)

    def to_vt(c, x):
        vt[:, pl.ds(pl.multiple_of(c * BLOCK, BLOCK), BLOCK)] = x.T.astype(BF16)

    def take0(c, carry):
        to_vt(c, mom[0, c].astype(F32) - recv[0, c].astype(F32))
        return carry

    take(moves, take0, 0)

    part = near
    parts_of = live_slots // part
    part_rows = part * BLOCK

    def adjoint(t, into):
        prod = jnp.dot(
            vt[...], kmat[:, pl.ds(pl.multiple_of(t * part_rows, part_rows), part_rows)],
            preferred_element_type=F32,
        ).T.reshape(part, BLOCK, width)
        into[pl.ds(t * part, part)] = prod
        v[pl.ds(t * part, part)] = prod.astype(BF16)

    def solve_and_send(e):
        moves = exchange(e)
        for t, ready in ((2, moves[0][2:]), (0, moves[0][:1]), (1, moves[0][1:2])):
            prod = jnp.dot(
                kmat[pl.ds(t * part_rows, part_rows), :],
                v[...].reshape(rows, width), preferred_element_type=F32,
            )
            mom[e, pl.ds(t * part, part)] = prod.reshape(part, BLOCK, width).astype(BF16)
            for copy in ready:
                copy.start()
        return moves

    def mask_fracs():
        for f in range(nblocks // per):
            for c in range(live_slots):
                weight = (frac[c] == f).astype(F32) * alive[c]
                vm[f, pl.ds(c * BLOCK, BLOCK)] = v[c] * jnp.full((BLOCK, width), weight, F32).astype(BF16)

    def solve_states(into, begin, end):
        def one(i, carry):
            f = lax.div(i, in_frac)
            lhs = jnp.concatenate(
                [
                    jnp.concatenate([a[step_blocks * i + b, column[c]] for b in range(step_blocks)], axis=0)
                    for c in range(live_slots)
                ],
                axis=1,
            )
            prod = jnp.dot(lhs, vm[f], preferred_element_type=F32)
            into[f, pl.ds(lax.rem(i, in_frac) * step_blocks, step_blocks)] = prod.reshape(
                step_blocks, BLOCK, width
            ).astype(BF16)
            return carry

        lax.fori_loop(begin, end, one, 0)

    def adj_g(t, carry):
        adjoint(t, g)
        return carry

    lax.fori_loop(0, parts_of, adj_g, 0)
    moves = solve_and_send(1)
    mask_fracs()
    solve_states(src, 0, tiles - 1)
    gg = lax.fori_loop(0, live_slots, lambda c, acc: acc + fold(g[c] * g[c]), zero)

    def take1(c, acc):
        x = recv[1, c].astype(F32) - mom[1, c].astype(F32)
        d[c] = x
        to_vt(c, x)
        return acc + fold(x * x)

    dd = take(moves, take1, zero)

    def adj_h(t, carry):
        adjoint(t, h)
        return carry

    lax.fori_loop(0, parts_of, adj_h, 0)
    moves = solve_and_send(2)
    solve_states(src, tiles - 1, tiles)
    mask_fracs()

    def norms(c, acc):
        gh, hh = acc
        return gh + fold(g[c] * h[c]), hh + fold(h[c] * h[c])

    gh, hh = lax.fori_loop(0, live_slots, norms, (zero, zero))
    solve_states(out_ref, 0, tiles - 3)

    def take2(c, acc):
        de, ee = acc
        x = recv[2, c].astype(F32) - mom[2, c].astype(F32)
        return de + fold(d[c] * x), ee + fold(x * x)

    de, ee = take(moves, take2, (zero, zero))

    row = lax.broadcasted_iota(jnp.int32, (8, 128), 0)
    pack = jnp.zeros((8, 128), F32)
    for q, part in enumerate((gg, gh, hh, dd, de, ee)):
        pack = jnp.where(row == q, jnp.sum(part), pack)
    red1[mi] = pack
    copies = [
        pltpu.make_async_remote_copy(
            src_ref=red1.at[mi], dst_ref=red1.at[mi],
            send_sem=r1s.at[k - 1], recv_sem=r1r.at[k - 1],
            device_id={"mem": lax.rem(mi + k, members)}, device_id_type=MESH,
        )
        for k in range(1, members)
    ]
    for copy in copies:
        copy.start()
    solve_states(out_ref, tiles - 3, tiles - 2)
    for copy in copies:
        copy.wait()
    red2[gi] = jnp.sum(red1[...], axis=0)
    copies = [
        pltpu.make_async_remote_copy(
            src_ref=red2.at[gi], dst_ref=red2.at[gi],
            send_sem=r2s.at[k - 1], recv_sem=r2r.at[k - 1],
            device_id={"grp": lax.rem(gi + k, groups)}, device_id_type=MESH,
        )
        for k in range(1, groups)
    ]
    for copy in copies:
        copy.start()
    solve_states(out_ref, tiles - 2, tiles)
    for copy in copies:
        copy.wait()
    total = jnp.sum(red2[...], axis=0)
    gg, gh, hh, dd, de, ee = [total[q : q + 1, :] for q in range(6)]
    step1 = gg / (0.5 * dd + PENALTY * gg)
    keep = 1.0 - PENALTY * step1
    sq2 = keep * keep * gg + 2.0 * keep * step1 * gh + step1 * step1 * hh
    dd2 = keep * keep * dd + 2.0 * keep * step1 * de + step1 * step1 * ee
    step2 = sq2 / (0.5 * dd2 + PENALTY * sq2)
    alpha = step1 + step2 * keep
    beta = step1 * step2
    alpha_w = jnp.concatenate([alpha] * (width // 128), axis=1)
    beta_w = jnp.concatenate([beta] * (width // 128), axis=1)

    parts = width // 128

    def put(slot, c):
        for q in range(parts):
            lanes = pl.ds(q * 128, 128)
            ctl_ref[slot, pl.ds(q, BLOCK, stride=parts), :] = -(
                alpha * g[c, :, lanes] + beta * h[c, :, lanes]
            )

    for c in range(live_slots):
        put(c if c < 2 * near else full_slot(c), c)
    for k in range(CAPM):
        ctl_ref[2 * near + mi * CAPM + k] = jnp.zeros((parts * BLOCK, 128), F32)

    def final(i, carry):
        f, r = lax.div(i, per), lax.rem(i, per)
        out_ref[f, r] = (
            s0[i] - alpha_w * src[f, r].astype(F32) - beta_w * out_ref[f, r].astype(F32)
        ).astype(BF16)
        return carry

    lax.fori_loop(0, nblocks, final, 0)


def per_device(inverse, sources, slot_blocks):
    members = lax.axis_size("mem")
    groups = lax.axis_size("grp")
    fracs, order, width = sources.shape
    slots = slot_blocks.shape[1]
    per = order // BLOCK
    nblocks = fracs * per
    tiles = nblocks // 4
    live = slots - CAPM
    rows = live * BLOCK
    vmem = pltpu.VMEM
    dma = pltpu.SemaphoreType.DMA
    control, states = pl.pallas_call(
        functools.partial(kernel, (groups, members, tiles, CAP, slots)),
        out_shape=(
            jax.ShapeDtypeStruct((slots, BLOCK * width // 128, 128), F32),
            jax.ShapeDtypeStruct((fracs, per, BLOCK, width), BF16),
        ),
        in_specs=[
            pl.BlockSpec(memory_space=pltpu.SMEM),
            pl.BlockSpec(memory_space=pl.ANY),
            pl.BlockSpec(memory_space=pl.ANY),
        ],
        out_specs=(pl.BlockSpec(memory_space=pltpu.VMEM), pl.BlockSpec(memory_space=pltpu.VMEM)),
        scratch_shapes=[
            vmem((nblocks, per, BLOCK, BLOCK), BF16),
            vmem((rows, rows), BF16),
            vmem((fracs, per, BLOCK, width), BF16),
            vmem((nblocks, BLOCK, width), F32),
            vmem((live, BLOCK, width), BF16),
            vmem((width, rows), BF16),
            vmem((fracs, rows, width), BF16),
            vmem((live, BLOCK, width), F32),
            vmem((live, BLOCK, width), F32),
            vmem((live, BLOCK, width), F32),
            vmem((3, live, BLOCK, width), BF16),
            vmem((3, live, BLOCK, width), BF16),
            vmem((members, 8, 128), F32),
            vmem((groups, 8, 128), F32),
            dma((tiles,)),
            dma,
            dma((3, members + 1)),
            dma((3, members + 1)),
            dma((members - 1,)),
            dma((members - 1,)),
            dma((groups - 1,)),
            dma((groups - 1,)),
        ],
        compiler_params=pltpu.CompilerParams(
            collective_id=0, has_side_effects=True, vmem_limit_bytes=67_043_328
        ),
    )(
        slot_blocks[0],
        inverse.reshape(fracs, per, BLOCK, order),
        sources.reshape(fracs, per, BLOCK, width),
    )
    return (control.reshape(1, slots, BLOCK * width), states.reshape(fracs, order, width))


def solution(mesh):
    in_specs = (
        P(("grp", "mem"), None, None),
        P(("grp", "mem"), None, None),
        P(("grp", "mem"), None),
    )
    out_specs = (P(("grp", "mem"), None, None), P(("grp", "mem"), None, None))
    return jax.shard_map(
        per_device, mesh=mesh, in_specs=in_specs, out_specs=out_specs, check_vma=False
    )
```

profile of v0, /device:TPU:0, one launch (start us, length us, event | category | flops | bytes accessed | tf_op | source)
XLA Modules:
  0.0 79.0 jit_solution(8647835527655197206)
XLA Ops:
  0.6 73.4 %shard_map.50 = (f32[20,256,128]{2,1,0:T(8,128)}, bf16[2,16,128,256]{3,2,1,0:T(8,128)(2,1)}) custom-call(s32[20]{0:T(128)} %bitcast.9, bf16[2,16,128,2048]{3,2,1,0:T(8,128)(2,1)} %bitcast.5, bf16[2,16,128,256]{3,2,1,0:T(8,128)(2,1)} %bitcast.8), custom_call_target="tpu_custom_call" | custom-call | tf_op jit(solution)/shard_map/pallas_call | solution.py:318
  74.0 0.0 copy-start
  74.0 3.6 %copy.9 = f32[1,20,32768]{2,0,1:T(1,128)} copy(f32[1,20,32768]{2,0,1:T(1,128)} %bitcast.6) | data formatting | bytes 5242880
  77.7 0.0 copy-done
  77.7 1.3 %copy.10 = bf16[2,2048,256]{2,1,0:T(8,128)(2,1)} copy(bf16[2,2048,256]{2,1,0:T(8,128)(2,1)S(1)} %bitcast.7) | data formatting | bytes 4194304
Async XLA Ops:
  74.0 3.6 %copy-start = (bf16[2,16,128,256]{3,2,1,0:T(8,128)(2,1)S(1)}, bf16[2,16,128,256]{3,2,1,0:T(8,128)(2,1)}, u32[]{:S(2)}) copy-start(bf16[2,16,128,256]{3,2,1,0:T(8,128)(2,1)} %get-tuple-element.5) | copy-start | bytes 6291460
where the time goes:
time: 79.1 us; the launch traced here: 79 us
  Pallas kernels  73.4 us (93%)
  local copies, waits for them, and re-layouts  4.95 us (6%)
    pallas_call x1, Pallas kernels, per_device(): pl.pallas_call(functools.partial(kernel, (groups, members, tiles, CAP, sl...  73.4 us
    unnamed x4, local copies, waits for them, and re-layouts  4.95 us

commit v1 on v0

--- a/solution.py
+++ b/solution.py
@@ -318,8 +318,8 @@
     control, states = pl.pallas_call(
         functools.partial(kernel, (groups, members, tiles, CAP, slots)),
         out_shape=(
-            jax.ShapeDtypeStruct((slots, BLOCK * width // 128, 128), F32),
-            jax.ShapeDtypeStruct((fracs, per, BLOCK, width), BF16),
+            pltpu.VMEM((slots, BLOCK * width // 128, 128), F32),
+            pltpu.VMEM((fracs, per, BLOCK, width), BF16),
         ),
         in_specs=[
             pl.BlockSpec(memory_space=pltpu.SMEM),
@@ -352,7 +352,7 @@
             dma((groups - 1,)),
         ],
         compiler_params=pltpu.CompilerParams(
-            collective_id=0, has_side_effects=True, vmem_limit_bytes=67_043_328
+            collective_id=0, has_side_effects=True, vmem_limit_bytes=61_000_000
         ),
     )(
         slot_blocks[0],

time: 79.1 us -> 74.9 us (0.947)
  local copies, waits for them, and re-layouts: 4.95 us -> 2.81 us
  Pallas kernels: 73.4 us -> 71.3 us
    unnamed x4 -> x2, local copies, waits for them, and re-layouts: 4.95 us -> 2.81 us
    pallas_call x1, Pallas kernels: 73.4 us -> 71.3 us  [per_device(): pl.pallas_call(functools.partial(kernel, (groups, members, tiles, CAP, sl...]
where the time goes in v1:
time: 74.9 us; the launch traced here: 74.7 us
  Pallas kernels  71.3 us (95%)
  local copies, waits for them, and re-layouts  2.81 us (4%)
    pallas_call x1, Pallas kernels, per_device(): pl.pallas_call(functools.partial(kernel, (groups, members, tiles, CAP, sl...  71.3 us
    unnamed x2, local copies, waits for them, and re-layouts  2.81 us

profile of v1, /device:TPU:0, one launch (start us, length us, event | category | flops | bytes accessed | tf_op | source)
XLA Modules:
  0.0 74.7 jit_solution(8876514759292433051)
XLA Ops:
  0.6 71.3 %shard_map.50 = (f32[20,256,128]{2,1,0:T(8,128)S(1)}, bf16[2,16,128,256]{3,2,1,0:T(8,128)(2,1)S(1)}) custom-call(s32[20]{0:T(128)} %bitcast.9, bf16[2,16,128,2048]{3,2,1,0:T(8,128)(2,1)} %bitcast.7, bf16[2,16,128,256]{3,2,1,0:T(8,128)(2,1)} %bitcast.8), custom_call_target="tpu_custom_call" | custom-call | tf_op jit(solution)/shard_map/pallas_call | solution.py:318
  71.9 1.5 %copy.9 = f32[1,20,32768]{2,0,1:T(1,128)} copy(f32[1,20,32768]{2,0,1:T(1,128)S(1)} %bitcast.5) | data formatting | bytes 5242880
  73.4 1.3 %copy.10 = bf16[2,2048,256]{2,1,0:T(8,128)(2,1)} copy(bf16[2,2048,256]{2,1,0:T(8,128)(2,1)S(1)} %bitcast.6) | data formatting | bytes 4194304

commit v2 on v1

v2 whole, which is shorter than its diff:
```python
import functools

import jax
import jax.numpy as jnp
from jax import lax
from jax.experimental import pallas as pl
from jax.experimental.pallas import tpu as pltpu
from jax.sharding import PartitionSpec as P

BLOCK = 128
CAP = 6
CAPM = 2
PENALTY = 0.5
HALVES = 2
F32 = jnp.float32
BF16 = jnp.bfloat16
MESH = pl.DeviceIdType.MESH


G1, G2, H1 = 3, 7, 4


def kernel(
    sizes, table, inv_hbm, src_hbm, g, out_h,
    a, kmat, kmat_t, out_g, s0, h, vt, vg, vm, mom, recv, red,
    load_sem, src_sem, send_sem, recv_sem, red_send, red_recv,
):
    groups, members, tiles, near, slots, halves = sizes
    width = s0.shape[2]
    half = width // halves
    nblocks, per = a.shape[:2]
    src = out_g
    order = per * BLOCK
    live_slots = slots - CAPM
    rows = live_slots * BLOCK
    gi = lax.axis_index("grp")
    mi = lax.axis_index("mem")

    step_blocks = nblocks // tiles
    in_frac = per // step_blocks

    src_copy = pltpu.make_async_copy(src_hbm, src, src_sem)
    src_copy.start()

    def load(i, carry):
        f, r = lax.div(i, in_frac), lax.rem(i, in_frac)
        for j in range(per):
            pltpu.make_async_copy(
                inv_hbm.at[f, pl.ds(r * step_blocks, step_blocks), :, pl.ds(j * BLOCK, BLOCK)],
                a.at[pl.ds(i * step_blocks, step_blocks), j],
                load_sem.at[i],
            ).start()
        return carry

    lax.fori_loop(0, tiles, load, 0)

    barrier = pltpu.get_barrier_semaphore()
    devices = groups * members
    me = gi * members + mi

    def peer(k):
        at = lax.rem(me + k, devices)
        return {"grp": lax.div(at, members), "mem": lax.rem(at, members)}

    def greet(k, carry):
        pl.semaphore_signal(barrier, inc=1, device_id=peer(k), device_id_type=MESH)
        return carry

    lax.fori_loop(1, devices, greet, 0)

    def full_slot(c):
        j = (c - 2 * near) // CAPM
        k = (c - 2 * near) % CAPM
        return 2 * near + lax.rem(mi + 1 + j, members) * CAPM + k

    names = []
    for c in range(live_slots):
        names.append(table[c] if c < 2 * near else table[full_slot(c)])
    place = [jnp.maximum(t, 0) for t in names]
    frac = [lax.div(t, per) for t in place]
    column = [t - f * per for t, f in zip(place, frac)]
    alive = [(t >= 0).astype(F32) for t in names]

    ahead = {"grp": lax.rem(gi + 1, groups)}
    behind = {"grp": lax.rem(gi + groups - 1, groups)}
    near_half = near // 2
    mem_half = CAPM // 2

    def offset(j):
        return 2 * near + j * CAPM

    def low(j):
        return lax.div(mi + 1 + j, members)

    def exchange(e, hf):
        if e < 2:
            plan = [(0, near, near, ahead), (near, 0, near, behind)]
            landed = [(near, near), (0, near)]
        else:
            plan = [(0, near, near_half, ahead), (near + near_half, near_half, near - near_half, behind)]
            landed = [(near, near_half), (near_half, near - near_half)]
        for j in range(members - 1):
            back = members - 2 - j
            device = {"mem": lax.rem(mi + 1 + j, members)}
            if e < 2:
                plan.append((offset(j), offset(back), CAPM, device))
                landed.append((offset(back), CAPM))
            else:
                at = low(j) * mem_half
                plan.append((offset(j) + at, offset(back) + at, mem_half, device))
                landed.append((offset(back) + (1 - low(back)) * mem_half, mem_half))
        copies = []
        for i, (at, to, count, device) in enumerate(plan):
            copies.append(pltpu.make_async_remote_copy(
                src_ref=mom.at[e % 2, hf, pl.ds(at, count)],
                dst_ref=recv.at[e % 2, hf, pl.ds(to, count)],
                send_sem=send_sem.at[e, hf, i],
                recv_sem=recv_sem.at[e, hf, i],
                device_id=device,
                device_id_type=MESH,
            ))
        return copies, landed

    def take(moves, one, carry):
        copies, landed = moves
        for i in (0, 1, *range(2, members + 1)):
            copies[i].wait()
            at, count = landed[i]
            for k in range(count):
                carry = one(at + k, carry)
        return carry

    src_copy.wait()

    def first(i, carry):
        whole = a.at[pl.ds(i * step_blocks, step_blocks)]
        pltpu.make_async_copy(whole, whole, load_sem.at[i]).wait()
        f = lax.div(i, in_frac)
        lhs = jnp.concatenate(
            [
                a[pl.ds(i * step_blocks, step_blocks), j].reshape(step_blocks * BLOCK, BLOCK)
                for j in range(per)
            ],
            axis=1,
        )
        prod = jnp.dot(lhs, src[f].reshape(order, width), preferred_element_type=F32)
        s0[pl.ds(i * step_blocks, step_blocks)] = prod.reshape(step_blocks, BLOCK, width)
        return carry

    lax.fori_loop(0, tiles, first, 0)

    def extract(hf, c):
        x = s0[place[c], :, pl.ds(hf * half, half)]
        mom[0, hf, c] = (x * alive[c]).T.astype(BF16)

    starts = []
    for hf in range(halves):
        moves = exchange(0, hf)
        for c in range(2 * near, live_slots):
            extract(hf, c)
        if hf == 0:
            pl.semaphore_wait(barrier, devices - 1)
        for copy in moves[0][2:]:
            copy.start()
        for c in range(2 * near):
            extract(hf, c)
        for copy in moves[0][:2]:
            copy.start()
        starts.append(moves)

    for r in range(live_slots):
        for c in range(live_slots):
            weight = (frac[r] == frac[c]).astype(F32) * alive[r] * alive[c]
            x = a[place[r], column[c]] * jnp.full((BLOCK, BLOCK), weight, F32).astype(BF16)
            kmat[pl.ds(r * BLOCK, BLOCK), pl.ds(c * BLOCK, BLOCK)] = x
            kmat_t[pl.ds(c * BLOCK, BLOCK), pl.ds(r * BLOCK, BLOCK)] = x.T

    def fold(x):
        return jnp.sum(x.reshape(x.shape[0] // 8, 8, x.shape[1]), axis=0)

    zero = jnp.zeros((8, 128), F32)
    small = jnp.zeros((8, BLOCK), F32)
    part = near
    parts_of = live_slots // part
    part_rows = part * BLOCK
    flipped = (((1,), (1,)), ((), ()))

    def adjoint(hf, into):
        for t in range(parts_of):
            prod = jnp.dot(
                vt[hf], kmat[:, pl.ds(t * part_rows, part_rows)], preferred_element_type=F32
            )
            vg[hf, :, pl.ds(t * part_rows, part_rows)] = prod.astype(BF16)
            for k in range(part):
                c = t * part + k
                x = prod[:, k * BLOCK : (k + 1) * BLOCK].T
                slot = c if c < 2 * near else full_slot(c)
                for q in range(half // 128):
                    into[slot, pl.ds(hf * (half // 128) + q, BLOCK, stride=width // 128), :] = x[
                        :, q * 128 : (q + 1) * 128
                    ]

    def solve_and_send(e, hf):
        moves = exchange(e, hf)
        copies = moves[0]
        for t, ready in ((2, copies[2:]), (0, copies[:1]), (1, copies[1:2])):
            prod = jnp.dot(
                vg[hf], kmat_t[:, pl.ds(t * part_rows, part_rows)], preferred_element_type=F32
            )
            for k in range(part):
                mom[e % 2, hf, t * part + k] = prod[:, k * BLOCK : (k + 1) * BLOCK].astype(BF16)
            for copy in ready:
                copy.start()
        return moves

    def mask_fracs(hf):
        for f in range(nblocks // per):
            for c in range(live_slots):
                weight = (frac[c] == f).astype(F32) * alive[c]
                cols = pl.ds(c * BLOCK, BLOCK)
                vm[f, pl.ds(hf * half, half), cols] = vg[hf, :, cols] * jnp.full(
                    (half, BLOCK), weight, F32
                ).astype(BF16)

    def solve_states(into, begin, end):
        def one(i, carry):
            f = lax.div(i, in_frac)
            lhs = jnp.concatenate(
                [
                    jnp.concatenate([a[step_blocks * i + b, column[c]] for b in range(step_blocks)], axis=0)
                    for c in range(live_slots)
                ],
                axis=1,
            )
            prod = lax.dot_general(lhs, vm[f], flipped, preferred_element_type=F32)
            into[f, pl.ds(lax.rem(i, in_frac) * step_blocks, step_blocks)] = prod.reshape(
                step_blocks, BLOCK, width
            ).astype(BF16)
            return carry

        if end > begin:
            lax.fori_loop(begin, end, one, 0)

    for k in range(CAPM):
        for into in (g, h):
            into[2 * near + mi * CAPM + k] = jnp.zeros(into.shape[1:], F32)

    second = []
    for hf in range(halves):

        def take0(c, carry):
            vt[hf, :, pl.ds(c * BLOCK, BLOCK)] = (mom[0, hf, c].astype(F32) - recv[0, hf, c].astype(F32)).astype(BF16)
            return carry

        take(starts[hf], take0, 0)
        adjoint(hf, g)
        second.append(solve_and_send(1, hf))
        mask_fracs(hf)

    solve_states(out_g, 0, G1)

    third = []
    dd = small
    for hf in range(halves):

        def take1(c, acc):
            x = recv[1, hf, c].astype(F32) - mom[1, hf, c].astype(F32)
            vt[hf, :, pl.ds(c * BLOCK, BLOCK)] = x.astype(BF16)
            return acc + fold(x * x)

        dd = take(second[hf], take1, dd)
        adjoint(hf, h)
        third.append(solve_and_send(2, hf))
        if hf == 0:
            solve_states(out_g, G1, G2)

    solve_states(out_g, G2, tiles)
    for hf in range(halves):
        mask_fracs(hf)
    solve_states(out_h, 0, H1)

    def norms(c, acc):
        gg, gh, hh = acc
        x, y = g[c], h[c]
        return gg + fold(x * x), gh + fold(x * y), hh + fold(y * y)

    gg, gh, hh = lax.fori_loop(0, slots, norms, (zero, zero, zero))

    kk = small
    for hf in range(halves):
        for c in range(live_slots):
            x = mom[0, hf, c].astype(F32)
            kk = kk + fold(x * x)
    cross = small
    for hf in range(halves):

        def take2(c, acc):
            return acc + fold(recv[0, hf, c].astype(F32) * mom[0, hf, c].astype(F32))

        cross = take(third[hf], take2, cross)

    lane = lax.broadcasted_iota(jnp.int32, (8, 128), 1)
    pack = jnp.zeros((8, 128), F32)
    for q, value in enumerate((gg, gh, hh, dd, kk - 2.0 * cross)):
        pack = jnp.where(lane == q, jnp.sum(value, axis=1, keepdims=True), pack)
    red[me] = jnp.sum(pack, axis=0, keepdims=True)

    def share(k):
        return pltpu.make_async_remote_copy(
            src_ref=red.at[me], dst_ref=red.at[me],
            send_sem=red_send.at[k - 1], recv_sem=red_recv.at[k - 1],
            device_id=peer(k), device_id_type=MESH,
        )

    def share_start(k, carry):
        share(k).start()
        return carry

    def share_wait(k, carry):
        share(k).wait()
        return carry

    lax.fori_loop(1, devices, share_start, 0)
    solve_states(out_h, H1, tiles)
    lax.fori_loop(1, devices, share_wait, 0)
    total = jnp.sum(red[...], axis=0)
    gg, gh, hh, dd, kk = [
        jnp.sum(jnp.where(lane[:1] == q, total, 0.0), axis=1, keepdims=True) for q in range(5)
    ]
    de, ee = -2.0 * hh, 2.0 * kk
    step1 = gg / (0.5 * dd + PENALTY * gg)
    keep = 1.0 - PENALTY * step1
    sq2 = keep * keep * gg + 2.0 * keep * step1 * gh + step1 * step1 * hh
    dd2 = jnp.maximum(keep * keep * dd + 2.0 * keep * step1 * de + step1 * step1 * ee, 0.0)
    step2 = sq2 / (0.5 * dd2 + PENALTY * sq2)
    alpha = step1 + step2 * keep
    beta = step1 * step2

    def controls(slot, carry):
        g[slot] = -(alpha * g[slot] + beta * h[slot])
        return carry

    lax.fori_loop(0, slots, controls, 0)

    def states(i, carry):
        f, r = lax.div(i, per), lax.rem(i, per)
        out_h[f, r] = (
            s0[i] - alpha * out_g[f, r].astype(F32) - beta * out_h[f, r].astype(F32)
        ).astype(BF16)
        return carry

    lax.fori_loop(0, nblocks, states, 0)


def per_device(inverse, sources, slot_blocks):
    members = lax.axis_size("mem")
    groups = lax.axis_size("grp")
    fracs, order, width = sources.shape
    slots = slot_blocks.shape[1]
    per = order // BLOCK
    nblocks = fracs * per
    tiles = nblocks // 4
    live = slots - CAPM
    rows = live * BLOCK
    halves = HALVES
    half = width // halves
    vmem = pltpu.VMEM
    dma = pltpu.SemaphoreType.DMA
    control, states = pl.pallas_call(
        functools.partial(kernel, (groups, members, tiles, CAP, slots, halves)),
        out_shape=(
            vmem((slots, BLOCK * width // 128, 128), F32),
            vmem((fracs, per, BLOCK, width), BF16),
        ),
        in_specs=[
            pl.BlockSpec(memory_space=pltpu.SMEM),
            pl.BlockSpec(memory_space=pl.ANY),
            pl.BlockSpec(memory_space=pl.ANY),
        ],
        out_specs=(pl.BlockSpec(memory_space=pltpu.VMEM),) * 2,
        scratch_shapes=[
            vmem((nblocks, per, BLOCK, BLOCK), BF16),
            vmem((rows, rows), BF16),
            vmem((rows, rows), BF16),
            vmem((fracs, per, BLOCK, width), BF16),
            vmem((nblocks, BLOCK, width), F32),
            vmem((slots, BLOCK * width // 128, 128), F32),
            vmem((halves, half, rows), BF16),
            vmem((halves, half, rows), BF16),
            vmem((fracs, width, rows), BF16),
            vmem((2, halves, live, half, BLOCK), BF16),
            vmem((2, halves, live, half, BLOCK), BF16),
            vmem((groups * members, 1, 128), F32),
            dma((tiles,)),
            dma,
            dma((3, halves, members + 1)),
            dma((3, halves, members + 1)),
            dma((groups * members - 1,)),
            dma((groups * members - 1,)),
        ],
        compiler_params=pltpu.CompilerParams(
            collective_id=0, has_side_effects=True, vmem_limit_bytes=61_500_000
        ),
    )(
        slot_blocks[0],
        inverse.reshape(fracs, per, BLOCK, order),
        sources.reshape(fracs, per, BLOCK, width),
    )
    return (control.reshape(1, slots, BLOCK * width), states.reshape(fracs, order, width))


def solution(mesh):
    in_specs = (
        P(("grp", "mem"), None, None),
        P(("grp", "mem"), None, None),
        P(("grp", "mem"), None),
    )
    out_specs = (P(("grp", "mem"), None, None), P(("grp", "mem"), None, None))
    return jax.shard_map(
        per_device, mesh=mesh, in_specs=in_specs, out_specs=out_specs, check_vma=False
    )
```

time: 74.9 us -> 63.3 us (0.85)
  Pallas kernels: 71.3 us -> 59.7 us
    pallas_call x1, Pallas kernels: 71.3 us -> 59.7 us  [per_device(): pl.pallas_call(functools.partial(kernel, (groups, members, tiles, CAP, sl...]
where the time goes in v2:
time: 63.3 us; the launch traced here: 63.2 us
  Pallas kernels  59.7 us (94%)
  local copies, waits for them, and re-layouts  2.81 us (4%)
  between operations  0.64 us (1%)
    pallas_call x1, Pallas kernels, per_device(): pl.pallas_call(functools.partial(kernel, (groups, members, tiles, CAP, sl...  59.7 us
    unnamed x2, local copies, waits for them, and re-layouts  2.81 us

profile of v2, /device:TPU:0, one launch (start us, length us, event | category | flops | bytes accessed | tf_op | source)
XLA Modules:
  0.0 63.2 jit_solution(6537627895512657735)
XLA Ops:
  0.6 59.7 %shard_map.50 = (f32[20,256,128]{2,1,0:T(8,128)S(1)}, bf16[2,16,128,256]{3,2,1,0:T(8,128)(2,1)S(1)}) custom-call(s32[20]{0:T(128)} %bitcast.9, bf16[2,16,128,2048]{3,2,1,0:T(8,128)(2,1)} %bitcast.7, bf16[2,16,128,256]{3,2,1,0:T(8,128)(2,1)} %bitcast.8), custom_call_target="tpu_custom_call" | custom-call | tf_op jit(solution)/shard_map/pallas_call | solution.py:369
  60.3 1.5 %copy.9 = f32[1,20,32768]{2,0,1:T(1,128)} copy(f32[1,20,32768]{2,0,1:T(1,128)S(1)} %bitcast.5) | data formatting | bytes 5242880
  61.8 1.3 %copy.10 = bf16[2,2048,256]{2,1,0:T(8,128)(2,1)} copy(bf16[2,2048,256]{2,1,0:T(8,128)(2,1)S(1)} %bitcast.6) | data formatting | bytes 4194304

commit v3 on v2

--- a/solution.py
+++ b/solution.py
@@ -17,7 +17,7 @@
 MESH = pl.DeviceIdType.MESH
 
 
-G1, G2, H1 = 3, 7, 4
+G1, G2, H1 = 2, 4, 2
 
 
 def kernel(
@@ -279,12 +279,16 @@
         mask_fracs(hf)
     solve_states(out_h, 0, H1)
 
-    def norms(c, acc):
+    together = 4 if slots % 4 == 0 else 1
+
+    def norms(i, acc):
         gg, gh, hh = acc
-        x, y = g[c], h[c]
-        return gg + fold(x * x), gh + fold(x * y), hh + fold(y * y)
-
-    gg, gh, hh = lax.fori_loop(0, slots, norms, (zero, zero, zero))
+        for k in range(together):
+            x, y = g[together * i + k], h[together * i + k]
+            gg, gh, hh = gg + fold(x * x), gh + fold(x * y), hh + fold(y * y)
+        return gg, gh, hh
+
+    gg, gh, hh = lax.fori_loop(0, slots // together, norms, (zero, zero, zero))
 
     kk = small
     for hf in range(halves):
@@ -336,20 +340,22 @@
     alpha = step1 + step2 * keep
     beta = step1 * step2
 
-    def controls(slot, carry):
-        g[slot] = -(alpha * g[slot] + beta * h[slot])
-        return carry
-
-    lax.fori_loop(0, slots, controls, 0)
-
-    def states(i, carry):
-        f, r = lax.div(i, per), lax.rem(i, per)
-        out_h[f, r] = (
-            s0[i] - alpha * out_g[f, r].astype(F32) - beta * out_h[f, r].astype(F32)
-        ).astype(BF16)
-        return carry
-
-    lax.fori_loop(0, nblocks, states, 0)
+    def controls(i, carry):
+        for k in range(together):
+            slot = together * i + k
+            g[slot] = -(alpha * g[slot] + beta * h[slot])
+        return carry
+
+    lax.fori_loop(0, slots // together, controls, 0)
+
+    def states(r, carry):
+        for f in range(nblocks // per):
+            out_h[f, r] = (
+                s0[f * per + r] - alpha * out_g[f, r].astype(F32) - beta * out_h[f, r].astype(F32)
+            ).astype(BF16)
+        return carry
+
+    lax.fori_loop(0, per, states, 0)
 
 
 def per_device(inverse, sources, slot_blocks):

time: 63.3 us -> 61.4 us (0.970)
  Pallas kernels: 59.7 us -> 57.8 us
    pallas_call x1, Pallas kernels: 59.7 us -> 57.8 us  [per_device(): pl.pallas_call(functools.partial(kernel, (groups, members, tiles, CAP, sl...]
where the time goes in v3:
time: 61.4 us; the launch traced here: 61.3 us
  Pallas kernels  57.8 us (94%)
  local copies, waits for them, and re-layouts  2.81 us (5%)
  between operations  0.64 us (1%)
    pallas_call x1, Pallas kernels, per_device(): pl.pallas_call(functools.partial(kernel, (groups, members, tiles, CAP, sl...  57.8 us
    unnamed x2, local copies, waits for them, and re-layouts  2.81 us

profile of v3, /device:TPU:0, one launch (start us, length us, event | category | flops | bytes accessed | tf_op | source)
XLA Modules:
  0.0 61.3 jit_solution(13594093199849266702)
XLA Ops:
  0.6 57.8 %shard_map.50 = (f32[20,256,128]{2,1,0:T(8,128)S(1)}, bf16[2,16,128,256]{3,2,1,0:T(8,128)(2,1)S(1)}) custom-call(s32[20]{0:T(128)} %bitcast.9, bf16[2,16,128,2048]{3,2,1,0:T(8,128)(2,1)} %bitcast.7, bf16[2,16,128,256]{3,2,1,0:T(8,128)(2,1)} %bitcast.8), custom_call_target="tpu_custom_call" | custom-call | tf_op jit(solution)/shard_map/pallas_call | solution.py:375
  58.4 1.5 %copy.9 = f32[1,20,32768]{2,0,1:T(1,128)} copy(f32[1,20,32768]{2,0,1:T(1,128)S(1)} %bitcast.5) | data formatting | bytes 5242880
  59.9 1.3 %copy.10 = bf16[2,2048,256]{2,1,0:T(8,128)(2,1)} copy(bf16[2,2048,256]{2,1,0:T(8,128)(2,1)S(1)} %bitcast.6) | data formatting | bytes 4194304
